TPU v7x, 32 devices: a whole 2x2x4 slice. The times are simulated.
32 devices in a mesh: group: 4 (over y, core), rep: 8 (over z, x).
Axes of the slice: x: 2, y: 2, z: 4, core: 2. Of those that a mesh axis runs over, the one named last changes fastest.
Arguments:
- table_hot: bfloat16 [32768, 512], P(('group', 'rep')), may hold values from -6 to 6
- table_mid: bfloat16 [131072, 128], P(('group', 'rep')), may hold values from -6 to 6
- table_cold: bfloat16 [131072, 128], P(('group', 'rep')), may hold values from -6 to 6
- proj_hot: bfloat16 [512, 256], replicated, may hold values from -0.25 to 0.25
- proj_mid: bfloat16 [128, 256], replicated, may hold values from -0.5 to 0.5
- proj_cold: bfloat16 [32, 256], replicated, may hold values from -1 to 1
- tower_in: bfloat16 [256, 1024], replicated, may hold values from -0.375 to 0.375
- tower_out: bfloat16 [1024, 256], replicated, may hold values from -0.1875 to 0.1875
- queries: bfloat16 [16384, 256], P(('group', 'rep')), may hold values from -68 to 68
- labels: int32 [16384], P(('group', 'rep')), may hold values from 0 to 4095
- item_slot: int32 [32, 4, 1024], P(('group', 'rep')), may hold values from 0 to 255
- item_block: int32 [32, 4, 1024], P(('group', 'rep')), may hold values from 0 to 2
- serve_rows: int32 [32, 3, 256], P(('group', 'rep')), may hold values from 0 to 16383, as said below
Outputs:
- query_loss: float32 [16384], P(('group', 'rep'))
- query_grad: float32 [16384, 256], P(('group', 'rep'))
- grad_hot: float32 [32768, 512], P(('group', 'rep'))
- grad_mid: float32 [131072, 128], P(('group', 'rep'))
- grad_cold: float32 [131072, 128], P(('group', 'rep'))
- grad_proj_hot: float32 [512, 256], P(None, 'rep')
- grad_proj_mid: float32 [128, 256], P(None, 'rep')
- grad_proj_cold: float32 [32, 256], P(None, 'rep')
- grad_tower_in: float32 [256, 1024], P(None, 'rep')
- grad_tower_out: float32 [1024, 256], P(None, 'rep')
Inputs may be any that keep to these rules, and one draw needn't show every extreme that they name: serve_rows[o, b, d * 8 + c] is a row of owner o's shard of block b that requester d sees in slot c; for block 0 it is below 1024, for block 1 below 4096, for block 2 below 16384; the 8 rows that one owner serves to one requester in one block are distinct.
All inputs are finite; a program needn't handle non-finite values.
Results may differ from a plain program's by a relative error of at most 0.02.
The roundings to bfloat16 on the way count: a program that leaves them out, or rounds other values in their place, can miss the bound.
Values may be sent and summed in bfloat16 or wider, within the bound.
No kernel may reach another device: no remote copies, remote signals or barrier semaphores. Data moves between devices by JAX's collectives and lax.ppermute only.
A program may use at most 128 MiB of HBM per device.

v0:
```python
import jax
import jax.numpy as jnp
from jax import lax
from jax.sharding import PartitionSpec as P

NORM_EPS = 1e-06
LOGIT_SCALE = 0.2


def merged(value, axis, join):
    pieces = jax.tree.map(lambda part: lax.all_gather(part, axis), value)
    head = jax.tree.map(lambda part: part[0], pieces)
    tail = jax.tree.map(lambda part: part[1:], pieces)
    total, _ = lax.scan(lambda total, piece: (join(total, piece), None), head, tail)
    return total


def silu_slope(pre_act):
    sigmoid = jax.nn.sigmoid(pre_act)
    return sigmoid * (1.0 + pre_act * (1.0 - sigmoid))


def pick_cold(cold_lines, row_ids, col_width):
    pieces = cold_lines.reshape(cold_lines.shape[0], 4, col_width)
    select = lax.broadcasted_iota(jnp.int32, (row_ids.shape[0], 4), 1) == (row_ids % 4)[:, None]
    return jnp.sum(jnp.where(select[:, :, None], pieces, jnp.zeros((), pieces.dtype)), axis=1)


def cold_add(row_ids, values, line_shape):
    select = (
        lax.broadcasted_iota(jnp.int32, (row_ids.shape[0], 4), 1) == (row_ids % 4)[:, None]
    ).astype(jnp.float32)
    spread = (select[:, :, None] * values[:, None, :]).reshape(row_ids.shape[0], line_shape[1])
    return jnp.zeros(line_shape, jnp.float32).at[row_ids // 4].add(spread)


def project(raw_rows, weight):
    return jnp.dot(raw_rows, weight, preferred_element_type=jnp.float32).astype(jnp.bfloat16)


def unproject(slot_grad, weight):
    return lax.dot_general(
        slot_grad, weight, (((1,), (1,)), ((), ())), preferred_element_type=jnp.float32
    )


def contract(left_rows, right_rows):
    return lax.dot_general(
        left_rows, right_rows, (((0,), (0,)), ((), ())), preferred_element_type=jnp.float32
    )


def combine_totals(earlier, later):
    joint_max = jnp.maximum(earlier[0], later[0])
    joint_sum = earlier[1] * jnp.exp(earlier[0] - joint_max) + later[1] * jnp.exp(
        later[0] - joint_max
    )
    return (joint_max, joint_sum, earlier[2] + later[2])


def local(
    table_hot,
    table_mid,
    table_cold,
    proj_hot,
    proj_mid,
    proj_cold,
    tower_in,
    tower_out,
    queries,
    labels,
    item_slot,
    item_block,
    serve_rows,
):
    devices = lax.axis_size(("group", "rep"))
    served = serve_rows[0]
    slot_total = served.shape[1]
    slots_each = slot_total // devices
    cold_width = proj_cold.shape[0]
    width_model = tower_in.shape[0]
    item_count = item_slot.shape[2]
    field_count = item_slot.shape[1]
    rows_hot = table_hot[served[0]]
    rows_mid = table_mid[served[1]]
    rows_cold = pick_cold(table_cold[served[2] // 4], served[2], cold_width)
    first_block = rows_hot.reshape(devices, slots_each, rows_hot.shape[1])
    got_first, got_mid, got_cold = (
        lax.all_to_all(first_block, ("group", "rep"), split_axis=0, concat_axis=0, tiled=True),
        lax.all_to_all(
            rows_mid.reshape(devices, slots_each, rows_mid.shape[1]),
            ("group", "rep"),
            split_axis=0,
            concat_axis=0,
            tiled=True,
        ),
        lax.all_to_all(
            rows_cold.reshape(devices, slots_each // 4, 4 * cold_width),
            ("group", "rep"),
            split_axis=0,
            concat_axis=0,
            tiled=True,
        ),
    )
    raw_mid = got_mid.reshape(slot_total, rows_mid.shape[1])
    raw_cold = got_cold.reshape(slot_total, cold_width)
    raw_hot = got_first.reshape(slot_total, rows_hot.shape[1])
    near_hot = project(raw_hot, proj_hot)
    slot_table = jnp.concatenate(
        [near_hot, project(raw_mid, proj_mid), project(raw_cold, proj_cold)], axis=0
    )
    slot_index = item_block[0] * slot_total + item_slot[0]
    pooled = jnp.sum(slot_table[slot_index].astype(jnp.float32), axis=0).astype(jnp.bfloat16)
    pre_act = jnp.dot(pooled, tower_in, preferred_element_type=jnp.float32)
    hidden = jax.nn.silu(pre_act).astype(jnp.bfloat16)
    residual = pooled.astype(jnp.float32) + jnp.dot(
        hidden, tower_out, preferred_element_type=jnp.float32
    )
    inv_rms = lax.rsqrt(jnp.mean(residual * residual, axis=1, keepdims=True) + NORM_EPS)
    vectors = (residual * inv_rms).astype(jnp.bfloat16)
    group_queries = lax.all_gather(queries, "group", axis=0, tiled=True)
    group_labels = lax.all_gather(labels, "group", axis=0, tiled=True)
    scores = (
        lax.dot_general(
            group_queries, vectors, (((1,), (1,)), ((), ())), preferred_element_type=jnp.float32
        )
        * LOGIT_SCALE
    )
    group_at = lax.axis_index("group")
    columns = group_at * item_count + lax.broadcasted_iota(jnp.int32, scores.shape, 1)
    onehot = columns == group_labels[:, None]
    local_max = jnp.max(scores, axis=1)
    local_total = jnp.sum(jnp.exp(scores - local_max[:, None]), axis=1)
    local_pick = jnp.sum(jnp.where(onehot, scores, 0.0), axis=1)
    joint_max, joint_sum, picked = merged(
        (local_max, local_total, local_pick), "group", combine_totals
    )
    log_total = joint_max + jnp.log(joint_sum)
    score_grad = (jnp.exp(scores - log_total[:, None]) - onehot.astype(jnp.float32)).astype(
        jnp.bfloat16
    )
    vec_grad = LOGIT_SCALE * contract(score_grad, group_queries)
    query_grad = lax.psum_scatter(
        (LOGIT_SCALE * jnp.dot(score_grad, vectors, preferred_element_type=jnp.float32)).astype(
            jnp.bfloat16
        ),
        "group",
        scatter_dimension=0,
        tiled=True,
    ).astype(jnp.float32)
    query_loss = lax.dynamic_slice_in_dim(
        log_total - picked, group_at * queries.shape[0], queries.shape[0], 0
    )
    dot_wide = jnp.sum(vec_grad * residual, axis=1, keepdims=True)
    wide_grad = inv_rms * vec_grad - inv_rms**3 / width_model * residual * dot_wide
    wide_low = wide_grad.astype(jnp.bfloat16)
    hidden_grad = unproject(wide_low, tower_out)
    pre_grad = (hidden_grad * silu_slope(pre_act)).astype(jnp.bfloat16)
    pooled_grad = (unproject(pre_grad, tower_in) + wide_grad).astype(jnp.bfloat16)
    stacked = jnp.broadcast_to(
        pooled_grad.astype(jnp.float32)[None], (field_count, item_count, width_model)
    ).reshape(-1, width_model)
    slot_grad = jax.ops.segment_sum(
        stacked, slot_index.reshape(-1), num_segments=3 * slot_total
    ).astype(jnp.bfloat16)
    grad_hot_slots = slot_grad[:slot_total]
    grad_mid_slots = slot_grad[slot_total : 2 * slot_total]
    grad_cold_slots = slot_grad[2 * slot_total :]
    grad_ph = contract(raw_hot, grad_hot_slots)
    back_hot, back_mid, back_cold = (
        lax.all_to_all(
            unproject(grad_hot_slots, proj_hot)
            .reshape(devices, slots_each, rows_hot.shape[1])
            .astype(jnp.bfloat16),
            ("group", "rep"),
            split_axis=0,
            concat_axis=0,
            tiled=True,
        ).astype(jnp.float32),
        lax.all_to_all(
            unproject(grad_mid_slots, proj_mid)
            .reshape(devices, slots_each, rows_mid.shape[1])
            .astype(jnp.bfloat16),
            ("group", "rep"),
            split_axis=0,
            concat_axis=0,
            tiled=True,
        ).astype(jnp.float32),
        lax.all_to_all(
            unproject(grad_cold_slots, proj_cold)
            .reshape(devices, slots_each // 4, 4 * cold_width)
            .astype(jnp.bfloat16),
            ("group", "rep"),
            split_axis=0,
            concat_axis=0,
            tiled=True,
        ).astype(jnp.float32),
    )
    back_hot = back_hot.reshape(slot_total, rows_hot.shape[1])
    grad_pm = contract(raw_mid, grad_mid_slots)
    grad_pc = contract(raw_cold, grad_cold_slots)
    grad_hot = jnp.zeros(table_hot.shape, jnp.float32).at[served[0]].add(back_hot)
    grad_mid = (
        jnp.zeros(table_mid.shape, jnp.float32)
        .at[served[1]]
        .add(back_mid.reshape(slot_total, rows_mid.shape[1]))
    )
    grad_cold = cold_add(served[2], back_cold.reshape(slot_total, cold_width), table_cold.shape)
    grad_in_local = contract(pooled, pre_grad)
    grad_out_local = contract(hidden, wide_low)
    totals = lax.psum((grad_ph, grad_pm, grad_pc, grad_in_local, grad_out_local), ("group", "rep"))
    rep_count = lax.axis_size("rep")
    rep_at = lax.axis_index("rep")
    summed = tuple(
        (
            lax.dynamic_slice_in_dim(
                full_sum,
                rep_at * (full_sum.shape[1] // rep_count),
                full_sum.shape[1] // rep_count,
                1,
            )
            for full_sum in totals
        )
    )
    return (
        query_loss,
        query_grad,
        grad_hot,
        grad_mid,
        grad_cold,
        summed[0],
        summed[1],
        summed[2],
        summed[3],
        summed[4],
    )


def solution(mesh):
    return jax.shard_map(
        local,
        mesh=mesh,
        in_specs=(
            P(("group", "rep"), None),
            P(("group", "rep"), None),
            P(("group", "rep"), None),
            P(),
            P(),
            P(),
            P(),
            P(),
            P(("group", "rep"), None),
            P(("group", "rep")),
            P(("group", "rep"), None, None),
            P(("group", "rep"), None, None),
            P(("group", "rep"), None, None),
        ),
        out_specs=(
            P(("group", "rep")),
            P(("group", "rep"), None),
            P(("group", "rep"), None),
            P(("group", "rep"), None),
            P(("group", "rep"), None),
            P(None, "rep"),
            P(None, "rep"),
            P(None, "rep"),
            P(None, "rep"),
            P(None, "rep"),
        ),
        check_vma=False,
    )
```

profile of v0, /device:TPU:0, one launch (start us, length us, event | category | flops | bytes accessed | tf_op | source)
XLA Modules:
  0.0 317.9 jit_solution(5360440472956101922)
XLA Ops:
  9.4 2.1 gather_fusion.2
  13.1 7.3 %all-to-all-start.2 = ((bf16[32,2,128]{2,1,0:T(2,128)(2,1)}), bf16[32,2,128]{2,1,0:T(2,128)(2,1)S(1)}, u32[]{:S(2)}, u32[]{:S(2)}) async-start(bf16[32,2,128]{2,1,0:T(2,128)(2,1)} %reshape.345), calls=%async_computation.2 | async-start | bytes 32768 | tf_op jit(solution)/shard_map/all_to_all | solution.py:97
  22.0 2.7 gather_fusion.1
  24.7 1.9 gather_fusion
  27.5 4.9 %all-to-all-start.1 = ((bf16[32,8,128]{2,1,0:T(8,128)(2,1)}), bf16[32,8,128]{2,1,0:T(8,128)(2,1)S(1)}, u32[]{:S(2)}, u32[]{:S(2)}) async-start(bf16[32,8,128]{2,1,0:T(8,128)(2,1)} %bitcast.9), calls=%async_computation.1 | async-start | bytes 131072 | tf_op jit(solution)/shard_map/all_to_all | solution.py:90
  33.0 6.7 %all-to-all-done.1 = bf16[32,8,128]{2,1,0:T(8,128)(2,1)S(1)} async-done(((bf16[32,8,128]{2,1,0:T(8,128)(2,1)}), bf16[32,8,128]{2,1,0:T(8,128)(2,1)S(1)}, u32[]{:S(2)}, u32[]{:S(2)}) %all-to-all-start.1) | async-done | bytes 65568 | tf_op jit(solution)/shard_map/all_to_all | solution.py:90
  39.7 2.6 all-to-all-start
  42.9 5.2 %all-gather.3 = s32[4,1,512]{2,1,0:T(1,128)S(1)} all-gather(s32[1,1,512]{2,1,0:T(1,128)S(1)} %bitcast.126), channel_id=1, replica_groups=mesh['group'=4,'rep'=8] {'group'}, dimensions={0}, use_global_device_ids=true | all-gather | bytes 10240 | tf_op jit(solution)/shard_map/all_gather | solution.py:122
  48.6 4.1 %all-to-all-done = bf16[32,8,512]{2,1,0:T(8,128)(2,1)S(1)} async-done(((bf16[32,8,512]{2,1,0:T(8,128)(2,1)}), bf16[32,8,512]{2,1,0:T(8,128)(2,1)S(1)}, u32[]{:S(2)}, u32[]{:S(2)}) %all-to-all-start) | async-done | bytes 262176 | tf_op jit(solution)/shard_map/all_to_all | solution.py:89
  53.4 16.6 %gather_fusion.3 = bf16[4096,256]{1,0:T(8,128)(2,1)S(1)} fusion(bf16[768,256]{1,0:T(8,128)(2,1)S(1)} %pad_maximum_fusion, s32[4096]{0:T(1024)} %bitcast_clamp_fusion), kind=kCustom, calls=%fused_computation.3 | custom fusion | bytes 4210688 | tf_op jit(solution)/shard_map/gather | solution.py:113
  72.5 4.5 %multiply_convert_fusion.1 = (bf16[1024,1024]{1,0:T(8,128)(2,1)S(1)}, f32[1024,1024]{1,0:T(8,128)}) fusion(bf16[1024,256]{1,0:T(8,128)(2,1)} %reduce_sum.61, bf16[256,1024]{1,0:T(8,128)(2,1)} %param.21), kind=kOutput, calls=%fused_computation.24 | convolution fusion | flops 542113792 | bytes 7340032 | tf_op jit(solution)/shard_map/dot_general | solution.py:114
  79.2 2.5 multiply_reduce_fusion
  81.7 5.2 %all-gather = f32[8192]{0:T(1024)S(1)} all-gather(f32[2048]{0:T(1024)S(1)} %get-tuple-element.88), channel_id=2, replica_groups=mesh['group'=4,'rep'=8] {'group'}, dimensions={0}, use_global_device_ids=true | all-gather | bytes 40960 | tf_op jit(solution)/shard_map/all_gather | solution.py:11
  86.9 2.7 fusion
  89.6 5.2 %all-gather.1 = f32[8192]{0:T(1024)S(1)} all-gather(f32[2048]{0:T(1024)S(1)} %get-tuple-element.53), channel_id=3, replica_groups=mesh['group'=4,'rep'=8] {'group'}, dimensions={0}, use_global_device_ids=true | all-gather | bytes 40960 | tf_op jit(solution)/shard_map/all_gather | solution.py:11
  94.8 5.4 %all-gather.2 = f32[8192]{0:T(1024)S(1)} all-gather(f32[2048]{0:T(1024)S(1)} %get-tuple-element.52), channel_id=4, replica_groups=mesh['group'=4,'rep'=8] {'group'}, dimensions={0}, use_global_device_ids=true | all-gather | bytes 40960 | tf_op jit(solution)/shard_map/all_gather | solution.py:11
  100.6 4.8 %fusion.2 = bf16[2048,1024]{0,1:T(8,128)(2,1)S(1)} fusion(f32[1024,2048]{1,0:T(8,128)} %copy-done.1, f32[2048]{0:T(1024)S(1)} %log_add_fusion, s32[2048]{0:T(1024)} %bitcast.117, s32[1024]{0:T(1024)S(1)} %iota_add_fusion), kind=kLoop, calls=%fused_computation.16 | loop fusion | flops 12582912 | bytes 12603392 | tf_op jit(solution)/shard_map/convert_element_type | solution.py:139
  109.1 1.9 multiply_convert_fusion
  117.0 3.5 %broadcast_in_dim.27 = f32[4,1024,256]{2,1,0:T(8,128)} broadcast(f32[1024,256]{1,0:T(8,128)} %copy.35), dimensions={1,2} | broadcast | bytes 5242880 | tf_op jit(solution)/shard_map/broadcast_in_dim | solution.py:160
  120.5 23.0 %scatter_custom_fusion = f32[768,256]{1,0:T(8,128)S(1)} fusion(s32[4096]{0:T(1024)} %bitcast.118, f32[4096,256]{1,0:T(8,128)} %bitcast.110, f32[]{:T(128)} %constant.85.clone.1), kind=kCustom, calls=%fused_computation.52 | custom fusion | flops 1048576 | bytes 786944 | tf_op jit(solution)/shard_map/scatter-add | solution.py:163
  146.5 4.6 %fusion.6 = bf16[2048,256]{1,0:T(8,128)(2,1)} fusion(bf16[2048,1024]{0,1:T(8,128)(2,1)} %copy-done.5, f32[1024,256]{0,1:T(8,128)S(1)} %get-tuple-element.87, f32[1024]{0:T(1024)S(1)} %get-tuple-element.78), kind=kOutput, calls=%fused_computation.27 | convolution fusion | flops 1075314688 | bytes 6295552 | tf_op jit(solution)/shard_map/dot_general | solution.py:144
  152.2 2.8 all-to-all-start.5
  155.8 6.2 %all-to-all-done.5 = bf16[32,2,128]{2,1,0:T(2,128)(2,1)S(1)} async-done(((bf16[32,2,128]{2,1,0:T(2,128)(2,1)}), bf16[32,2,128]{2,1,0:T(2,128)(2,1)S(1)}, u32[]{:S(2)}, u32[]{:S(2)}) %all-to-all-start.5) | async-done | bytes 16416 | tf_op jit(solution)/shard_map/all_to_all | solution.py:189
  162.0 2.6 all-to-all-start.4
  165.6 6.7 %all-to-all-done.4 = bf16[32,8,128]{2,1,0:T(8,128)(2,1)S(1)} async-done(((bf16[32,8,128]{2,1,0:T(8,128)(2,1)}), bf16[32,8,128]{2,1,0:T(8,128)(2,1)S(1)}, u32[]{:S(2)}, u32[]{:S(2)}) %all-to-all-start.4) | async-done | bytes 65568 | tf_op jit(solution)/shard_map/all_to_all | solution.py:180
  172.3 2.6 all-to-all-start.3
  175.1 40.9 %psum.37 = f32[32,256]{1,0:T(8,128)S(1)} all-reduce(f32[32,256]{1,0:T(8,128)S(1)} %fusion.27), channel_id=1, replica_groups=mesh['group'=4,'rep'=8] {'group','rep'}, use_global_device_ids=true, to_apply=%region_16.17 | all-reduce | flops 8192 | bytes 65536 | tf_op jit(solution)/shard_map/psum | solution.py:211
  218.3 3.0 scatter_custom_fusion.3
  221.3 3.0 scatter_custom_fusion.2
  224.2 3.7 %scatter_custom_fusion.1 = f32[1024,512]{1,0:T(8,128)} fusion(s32[256]{0:T(256)} %bitcast.120, f32[]{:T(128)} %constant.85.clone.1, bf16[32,8,512]{2,1,0:T(8,128)(2,1)S(1)} %all-to-all-done.3), kind=kCustom, calls=%fused_computation.46 | custom fusion | flops 262144 | bytes 2359808 | tf_op jit(solution)/shard_map/scatter-add | solution.py:202
  227.9 55.4 %all-reduce.3.cloned.1.call-done = (f32[512,256]{0,1:T(8,128)}, f32[128,256]{0,1:T(8,128)}, f32[256,1024]{1,0:T(8,128)}, f32[1024,256]{0,1:T(8,128)}) async-done(((f32[512,256]{0,1:T(8,128)}, f32[128,256]{0,1:T(8,128)}, f32[256,1024]{1,0:T(8,128)}, f32[1024,256]{0,1:T(8,128)}), (f32[512,256]{0,1:T(8,128)}, f32[128,256]{0,1:T(8,128)}, f32[256,1024]{1,0:T(8,128)}, ...) | async-done | bytes 2752528 | tf_op jit(solution)/shard_map/psum | solution.py:211
  289.2 20.4 %reduce-scatter.2.cloned.1.call-done = bf16[512,256]{1,0:T(8,128)(2,1)} async-done(((bf16[2048,256]{1,0:T(8,128)(2,1)}), bf16[512,256]{1,0:T(8,128)(2,1)}) %reduce-scatter.2.cloned.1.call-update) | async-done | bytes 262160 | tf_op jit(solution)/shard_map/reduce_scatter | solution.py:143
  (139 shorter events, 39.2 us)
Async XLA Ops:
  7.2 17.5 %copy-start = (bf16[1024,512]{1,0:T(8,128)(2,1)S(1)}, bf16[1024,512]{1,0:T(8,128)(2,1)}, u32[]{:S(2)}) copy-start(bf16[1024,512]{1,0:T(8,128)(2,1)} %param.15) | copy-start | bytes 3145732
  7.2 35.7 %copy-start.26 = (s32[512]{0:T(512)S(1)}, s32[512]{0:T(512)}, u32[]{:S(2)}) copy-start(s32[512]{0:T(512)} %param.24) | copy-start | bytes 6148
  7.2 41.0 %copy-start.20 = (bf16[32,256]{1,0:T(8,128)(2,1)S(1)}, bf16[32,256]{1,0:T(8,128)(2,1)}, u32[]{:S(2)}) copy-start(bf16[32,256]{1,0:T(8,128)(2,1)} %param.20) | copy-start | bytes 49156
  7.2 41.2 %copy-start.16 = (bf16[128,256]{1,0:T(8,128)(2,1)S(1)}, bf16[128,256]{1,0:T(8,128)(2,1)}, u32[]{:S(2)}) copy-start(bf16[128,256]{1,0:T(8,128)(2,1)} %param.19) | copy-start | bytes 196612
  7.2 45.5 %copy-start.9 = (bf16[512,256]{1,0:T(8,128)(2,1)S(1)}, bf16[512,256]{1,0:T(8,128)(2,1)}, u32[]{:S(2)}) copy-start(bf16[512,256]{1,0:T(8,128)(2,1)} %param.18) | copy-start | bytes 786436
  7.2 71.9 %all-gather.6.cloned.1.call-start = ((), (), s32[]{:S(2)}) async-start(), calls=%async_computation.7 | async-start | bytes 1310720 | tf_op jit(solution)/shard_map/all_gather | solution.py:121
  8.7 4.4 %copy-start.25 = (s32[256,1]{0,1:T(1,128)}, s32[256,1]{0,1:T(1,128)S(1)}, u32[]{:S(2)}) copy-start(s32[256,1]{0,1:T(1,128)S(1)} %get-tuple-element.80) | copy-start | bytes 3076
  8.7 13.2 %copy-start.24 = (s32[256,1]{0,1:T(1,128)}, s32[256,1]{0,1:T(1,128)S(1)}, u32[]{:S(2)}) copy-start(s32[256,1]{0,1:T(1,128)S(1)} %get-tuple-element.81) | copy-start | bytes 3076
  8.7 34.2 %copy-start.23 = (s32[256,1]{0,1:T(1,128)}, s32[256,1]{0,1:T(1,128)S(1)}, u32[]{:S(2)}) copy-start(s32[256,1]{0,1:T(1,128)S(1)} %get-tuple-element.79) | copy-start | bytes 3076
  13.1 14.4 %all-to-all-start.2 = ((bf16[32,2,128]{2,1,0:T(2,128)(2,1)}), bf16[32,2,128]{2,1,0:T(2,128)(2,1)S(1)}, u32[]{:S(2)}, u32[]{:S(2)}) async-start(bf16[32,2,128]{2,1,0:T(2,128)(2,1)} %reshape.345), calls=%async_computation.2 | async-start | bytes 32768 | tf_op jit(solution)/shard_map/all_to_all | solution.py:97
  27.5 12.2 %all-to-all-start.1 = ((bf16[32,8,128]{2,1,0:T(8,128)(2,1)}), bf16[32,8,128]{2,1,0:T(8,128)(2,1)S(1)}, u32[]{:S(2)}, u32[]{:S(2)}) async-start(bf16[32,8,128]{2,1,0:T(8,128)(2,1)} %bitcast.9), calls=%async_computation.1 | async-start | bytes 131072 | tf_op jit(solution)/shard_map/all_to_all | solution.py:90
  39.7 13.3 %copy-start.13 = (bf16[32,8,128]{2,1,0:T(8,128)(2,1)}, bf16[32,8,128]{2,1,0:T(8,128)(2,1)S(1)}, u32[]{:S(2)}) copy-start(bf16[32,8,128]{2,1,0:T(8,128)(2,1)S(1)} %all-to-all-done.1) | copy-start | bytes 196612
  39.7 13.0 %all-to-all-start = ((bf16[32,8,512]{2,1,0:T(8,128)(2,1)}), bf16[32,8,512]{2,1,0:T(8,128)(2,1)S(1)}, u32[]{:S(2)}, u32[]{:S(2)}) async-start(bf16[32,8,512]{2,1,0:T(8,128)(2,1)} %bitcast.5), calls=%async_computation | async-start | bytes 524288 | tf_op jit(solution)/shard_map/all_to_all | solution.py:89
  42.3 241.1 %all-reduce.3.cloned.1.call-start = ((), (), s32[]{:S(2)}) async-start(), calls=%async_computation.9 | async-start | bytes 5505024 | tf_op jit(solution)/shard_map/psum | solution.py:211
  48.1 38.8 %copy-start.18 = (s32[4,1,512]{2,1,0:T(1,128)}, s32[4,1,512]{2,1,0:T(1,128)S(1)}, u32[]{:S(2)}) copy-start(s32[4,1,512]{2,1,0:T(1,128)S(1)} %all-gather.3) | copy-start | bytes 24580
  48.2 4.7 %copy-start.11 = (bf16[256,32]{1,0:T(8,128)(2,1)}, bf16[256,32]{1,0:T(8,128)(2,1)S(1)}, u32[]{:S(2)}) copy-start(bf16[256,32]{1,0:T(8,128)(2,1)S(1)} %reshape.346) | copy-start | bytes 49156
  72.5 5.9 %copy-start.14 = (bf16[1024,256]{1,0:T(8,128)(2,1)S(1)}, bf16[1024,256]{1,0:T(8,128)(2,1)}, u32[]{:S(2)}) copy-start(bf16[1024,256]{1,0:T(8,128)(2,1)} %param.22) | copy-start | bytes 1572868
  81.7 7.9 %copy-start.1 = (f32[1024,2048]{1,0:T(8,128)}, f32[1024,2048]{1,0:T(8,128)S(1)}, u32[]{:S(2)}) copy-start(f32[1024,2048]{1,0:T(8,128)S(1)} %get-tuple-element.89) | copy-start | bytes 25165828
  100.6 4.8 %copy-start.19 = (f32[2048]{0:T(1024)}, f32[2048]{0:T(1024)S(1)}, u32[]{:S(2)}) copy-start(f32[2048]{0:T(1024)S(1)} %log_add_fusion) | copy-start | bytes 24580
  100.6 4.8 %copy-start.8 = (bf16[2048,256]{1,0:T(8,128)(2,1)S(1)}, bf16[2048,256]{1,0:T(8,128)(2,1)}, u32[]{:S(2)}) copy-start(bf16[2048,256]{1,0:T(8,128)(2,1)} %all-gather.6.cloned.1.call-done) | copy-start | bytes 3145732
  105.4 3.7 %copy-start.27 = (f32[1024,1024]{1,0:T(8,128)S(1)}, f32[1024,1024]{1,0:T(8,128)}, u32[]{:S(2)}) copy-start(f32[1024,1024]{1,0:T(8,128)} %get-tuple-element.85) | copy-start | bytes 12582916
  111.1 2.8 copy-start.3
  115.6 27.9 %copy-start.7 = (bf16[32,8,512]{2,1,0:T(8,128)(2,1)S(1)}, bf16[32,8,512]{2,1,0:T(8,128)(2,1)}, u32[]{:S(2)}) copy-start(bf16[32,8,512]{2,1,0:T(8,128)(2,1)} %copy-done.6) | copy-start | bytes 786436
  146.4 4.7 %copy-start.21 = (bf16[32,256]{1,0:T(8,128)(2,1)S(1)}, bf16[32,256]{1,0:T(8,128)(2,1)}, u32[]{:S(2)}) copy-start(bf16[32,256]{1,0:T(8,128)(2,1)} %param.20) | copy-start | bytes 49156
  146.4 8.5 %copy-start.17 = (bf16[128,256]{1,0:T(8,128)(2,1)S(1)}, bf16[128,256]{1,0:T(8,128)(2,1)}, u32[]{:S(2)}) copy-start(bf16[128,256]{1,0:T(8,128)(2,1)} %param.19) | copy-start | bytes 196612
  146.4 18.2 %copy-start.10 = (bf16[512,256]{1,0:T(8,128)(2,1)S(1)}, bf16[512,256]{1,0:T(8,128)(2,1)}, u32[]{:S(2)}) copy-start(bf16[512,256]{1,0:T(8,128)(2,1)} %param.18) | copy-start | bytes 786436
  146.4 28.5 %copy-start.12 = (bf16[256,32]{1,0:T(8,128)(2,1)S(1)}, bf16[256,32]{1,0:T(8,128)(2,1)}, u32[]{:S(2)}) copy-start(bf16[256,32]{1,0:T(8,128)(2,1)} %copy-done.11) | copy-start | bytes 49156
  146.5 71.7 %copy-start.22 = (f32[256,4]{0,1:T(4,128)S(1)}, f32[256,4]{0,1:T(4,128)}, u32[]{:S(2)}) copy-start(f32[256,4]{0,1:T(4,128)} %get-tuple-element.82) | copy-start | bytes 12292
  146.5 163.1 %reduce-scatter.2.cloned.1.call-start = ((), (), s32[]{:S(2)}) async-start(), calls=%async_computation.8 | async-start | bytes 1310720 | tf_op jit(solution)/shard_map/reduce_scatter | solution.py:143
  152.2 9.8 %all-to-all-start.5 = ((bf16[32,2,128]{2,1,0:T(2,128)(2,1)}), bf16[32,2,128]{2,1,0:T(2,128)(2,1)S(1)}, u32[]{:S(2)}, u32[]{:S(2)}) async-start(bf16[32,2,128]{2,1,0:T(2,128)(2,1)} %convert_element_type.98), calls=%async_computation.6 | async-start | bytes 32768 | tf_op jit(solution)/shard_map/all_to_all | solution.py:189
  162.0 10.3 %all-to-all-start.4 = ((bf16[32,8,128]{2,1,0:T(8,128)(2,1)}), bf16[32,8,128]{2,1,0:T(8,128)(2,1)S(1)}, u32[]{:S(2)}, u32[]{:S(2)}) async-start(bf16[32,8,128]{2,1,0:T(8,128)(2,1)} %fusion.10), calls=%async_computation.5 | async-start | bytes 131072 | tf_op jit(solution)/shard_map/all_to_all | solution.py:180
  172.3 51.9 %all-to-all-start.3 = ((bf16[32,8,512]{2,1,0:T(8,128)(2,1)}), bf16[32,8,512]{2,1,0:T(8,128)(2,1)S(1)}, u32[]{:S(2)}, u32[]{:S(2)}) async-start(bf16[32,8,512]{2,1,0:T(8,128)(2,1)} %fusion.9), calls=%async_computation.4 | async-start | bytes 524288 | tf_op jit(solution)/shard_map/all_to_all | solution.py:171
  (5 other events, 7.1 us)
Sparse Core Ops, SparseCore 0:
  9.6 19.5 all-gather.5
  146.5 136.7 all-reduce.2
  285.8 23.7 reduce-scatter.1
where the time goes:
time: 319 us; the launch traced here: 318 us
  waiting for transfers between devices  101 us (32%)
  blocking collectives  61.8 us (19%)
  other arithmetic  48.3 us (15%)
  local copies, waits for them, and re-layouts  43.6 us (14%)
  matrix products  25.5 us (8%)
  starting transfers between devices  22.8 us (7%)
  between operations  14.4 us (5%)
    psum x1, waiting for transfers between devices, local(): lax.psum((grad_ph, grad_pm, grad_pc, grad_in_local, grad_out_local), ('gr...  55.4 us
    psum x1, blocking collectives, local(): lax.psum((grad_ph, grad_pm, grad_pc, grad_in_local, grad_out_local), ('gr...  40.9 us
    scatter-add x1, other arithmetic, local(): jax.ops.segment_sum(stacked, slot_index.reshape(-1), num_segments=3 * slo...  23 us
    reduce_scatter x1, waiting for transfers between devices, local(): lax.psum_scatter((LOGIT_SCALE * jnp.dot(score_grad, vectors, preferred_el...  20.4 us
    gather x1, local copies, waits for them, and re-layouts, local(): slot_table[slot_index].astype(jnp.float32)  16.6 us
    all_gather x3, blocking collectives, merged(): pieces = jax.tree.map(lambda part: lax.all_gather(part, axis), value)  15.7 us
    dot_general x6, matrix products, contract(): lax.dot_general(left_rows, right_rows, (((0,), (0,)), ((), ())), preferre...  7.8 us
    all_to_all x1, starting transfers between devices, local(): lax.all_to_all(rows_cold.reshape(devices, slots_each // 4, 4 * cold_width...  7.33 us
  transfers between devices with their start and end apart: 9, of which 7 were waited for; matrix products, arithmetic and copies ran while one was open for 20% of the time, Pallas kernels for 0%

commit v1 on v0

--- a/solution.py
+++ b/solution.py
@@ -208,7 +208,9 @@
     grad_cold = cold_add(served[2], back_cold.reshape(slot_total, cold_width), table_cold.shape)
     grad_in_local = contract(pooled, pre_grad)
     grad_out_local = contract(hidden, wide_low)
-    totals = lax.psum((grad_ph, grad_pm, grad_pc, grad_in_local, grad_out_local), ("group", "rep"))
+    totals = (grad_ph, grad_pm, grad_pc, grad_in_local, grad_out_local)
+    for mesh_axis in ("rep", "group"):
+        totals = lax.psum(totals, mesh_axis)
     rep_count = lax.axis_size("rep")
     rep_at = lax.axis_index("rep")
     summed = tuple(

time: 319 us -> 368 us (1.15)
  waiting for transfers between devices: 101 us -> 142 us
  blocking collectives: 61.8 us -> 69.5 us
    psum x1 -> x2, waiting for transfers between devices: 55.4 us -> 117 us  [local(): totals = lax.psum(totals, mesh_axis)]
    reduce_scatter x1, waiting for transfers between devices: 20.4 us -> 0.01 us  [local(): lax.psum_scatter((LOGIT_SCALE * jnp.dot(score_grad, vectors, preferred_el...]
    psum x1 -> x2, blocking collectives: 40.9 us -> 48.6 us  [local(): totals = lax.psum(totals, mesh_axis)]
  transfers between devices with their start and end apart: 9 -> 10, of which waited for: 7 -> 7; matrix products, arithmetic and copies ran while one was open for 20% -> 16% of each run, Pallas kernels for 0% -> 0%
where the time goes in v1:
time: 368 us; the launch traced here: 367 us
  waiting for transfers between devices  142 us (39%)
  blocking collectives  69.5 us (19%)
  other arithmetic  48.3 us (13%)
  local copies, waits for them, and re-layouts  43.6 us (12%)
  matrix products  25.2 us (7%)
  starting transfers between devices  23.7 us (6%)
  between operations  14.4 us (4%)
    psum x2, waiting for transfers between devices, local(): totals = lax.psum(totals, mesh_axis)  117 us
    psum x2, blocking collectives, local(): totals = lax.psum(totals, mesh_axis)  48.6 us
    scatter-add x1, other arithmetic, local(): jax.ops.segment_sum(stacked, slot_index.reshape(-1), num_segments=3 * slo...  23 us
    gather x1, local copies, waits for them, and re-layouts, local(): slot_table[slot_index].astype(jnp.float32)  16.6 us
    all_gather x3, blocking collectives, merged(): pieces = jax.tree.map(lambda part: lax.all_gather(part, axis), value)  15.7 us
    dot_general x6, matrix products, contract(): lax.dot_general(left_rows, right_rows, (((0,), (0,)), ((), ())), preferre...  7.66 us
  transfers between devices with their start and end apart: 10, of which 7 were waited for; matrix products, arithmetic and copies ran while one was open for 16% of the time, Pallas kernels for 0%

profile of v1, /device:TPU:0, one launch (start us, length us, event | category | flops | bytes accessed | tf_op | source)
XLA Modules:
  0.0 367.0 jit_solution(16189390172835464637)
XLA Ops:
  9.4 2.1 gather_fusion.2
  13.1 7.3 %all-to-all-start.2 = ((bf16[32,2,128]{2,1,0:T(2,128)(2,1)}), bf16[32,2,128]{2,1,0:T(2,128)(2,1)S(1)}, u32[]{:S(2)}, u32[]{:S(2)}) async-start(bf16[32,2,128]{2,1,0:T(2,128)(2,1)} %reshape.345), calls=%async_computation.2 | async-start | bytes 32768 | tf_op jit(solution)/shard_map/all_to_all | solution.py:97
  22.0 2.7 gather_fusion.1
  27.5 4.9 %all-to-all-start.1 = ((bf16[32,8,128]{2,1,0:T(8,128)(2,1)}), bf16[32,8,128]{2,1,0:T(8,128)(2,1)S(1)}, u32[]{:S(2)}, u32[]{:S(2)}) async-start(bf16[32,8,128]{2,1,0:T(8,128)(2,1)} %bitcast.9), calls=%async_computation.1 | async-start | bytes 131072 | tf_op jit(solution)/shard_map/all_to_all | solution.py:90
  33.0 6.7 %all-to-all-done.1 = bf16[32,8,128]{2,1,0:T(8,128)(2,1)S(1)} async-done(((bf16[32,8,128]{2,1,0:T(8,128)(2,1)}), bf16[32,8,128]{2,1,0:T(8,128)(2,1)S(1)}, u32[]{:S(2)}, u32[]{:S(2)}) %all-to-all-start.1) | async-done | bytes 65568 | tf_op jit(solution)/shard_map/all_to_all | solution.py:90
  39.7 2.6 all-to-all-start
  42.9 5.2 %all-gather.3 = s32[4,1,512]{2,1,0:T(1,128)S(1)} all-gather(s32[1,1,512]{2,1,0:T(1,128)S(1)} %bitcast.126), channel_id=1, replica_groups=mesh['group'=4,'rep'=8] {'group'}, dimensions={0}, use_global_device_ids=true | all-gather | bytes 10240 | tf_op jit(solution)/shard_map/all_gather | solution.py:122
  48.6 4.1 %all-to-all-done = bf16[32,8,512]{2,1,0:T(8,128)(2,1)S(1)} async-done(((bf16[32,8,512]{2,1,0:T(8,128)(2,1)}), bf16[32,8,512]{2,1,0:T(8,128)(2,1)S(1)}, u32[]{:S(2)}, u32[]{:S(2)}) %all-to-all-start) | async-done | bytes 262176 | tf_op jit(solution)/shard_map/all_to_all | solution.py:89
  53.4 16.6 %gather_fusion.3 = bf16[4096,256]{1,0:T(8,128)(2,1)S(1)} fusion(bf16[768,256]{1,0:T(8,128)(2,1)S(1)} %pad_maximum_fusion, s32[4096]{0:T(1024)} %bitcast_clamp_fusion), kind=kCustom, calls=%fused_computation.3 | custom fusion | bytes 4210688 | tf_op jit(solution)/shard_map/gather | solution.py:113
  72.5 4.5 %multiply_convert_fusion.1 = (bf16[1024,1024]{1,0:T(8,128)(2,1)S(1)}, f32[1024,1024]{1,0:T(8,128)}) fusion(bf16[1024,256]{1,0:T(8,128)(2,1)} %reduce_sum.61, bf16[256,1024]{1,0:T(8,128)(2,1)} %param.21), kind=kOutput, calls=%fused_computation.24 | convolution fusion | flops 542113792 | bytes 7340032 | tf_op jit(solution)/shard_map/dot_general | solution.py:114
  79.1 2.5 multiply_reduce_fusion
  81.6 5.2 %all-gather = f32[8192]{0:T(1024)S(1)} all-gather(f32[2048]{0:T(1024)S(1)} %get-tuple-element.92), channel_id=2, replica_groups=mesh['group'=4,'rep'=8] {'group'}, dimensions={0}, use_global_device_ids=true | all-gather | bytes 40960 | tf_op jit(solution)/shard_map/all_gather | solution.py:11
  86.8 2.7 fusion
  89.5 5.2 %all-gather.1 = f32[8192]{0:T(1024)S(1)} all-gather(f32[2048]{0:T(1024)S(1)} %get-tuple-element.53), channel_id=3, replica_groups=mesh['group'=4,'rep'=8] {'group'}, dimensions={0}, use_global_device_ids=true | all-gather | bytes 40960 | tf_op jit(solution)/shard_map/all_gather | solution.py:11
  94.7 5.4 %all-gather.2 = f32[8192]{0:T(1024)S(1)} all-gather(f32[2048]{0:T(1024)S(1)} %get-tuple-element.52), channel_id=4, replica_groups=mesh['group'=4,'rep'=8] {'group'}, dimensions={0}, use_global_device_ids=true | all-gather | bytes 40960 | tf_op jit(solution)/shard_map/all_gather | solution.py:11
  100.5 4.8 %fusion.2 = bf16[2048,1024]{0,1:T(8,128)(2,1)S(1)} fusion(f32[1024,2048]{1,0:T(8,128)} %copy-done.1, f32[2048]{0:T(1024)S(1)} %log_add_fusion, s32[2048]{0:T(1024)} %bitcast.117, s32[1024]{0:T(1024)S(1)} %iota_add_fusion), kind=kLoop, calls=%fused_computation.16 | loop fusion | flops 12582912 | bytes 12603392 | tf_op jit(solution)/shard_map/convert_element_type | solution.py:139
  109.0 1.9 multiply_convert_fusion
  116.7 3.5 broadcast_in_dim.27
  120.3 23.0 %scatter_custom_fusion = f32[768,256]{1,0:T(8,128)S(1)} fusion(s32[4096]{0:T(1024)} %bitcast.118, f32[4096,256]{1,0:T(8,128)} %bitcast.110, f32[]{:T(128)} %constant.85.clone.1), kind=kCustom, calls=%fused_computation.52 | custom fusion | flops 1048576 | bytes 786944 | tf_op jit(solution)/shard_map/scatter-add | solution.py:163
  146.2 4.5 %fusion.6 = bf16[2048,256]{1,0:T(8,128)(2,1)} fusion(bf16[2048,1024]{0,1:T(8,128)(2,1)} %copy-done.5, f32[1024,256]{0,1:T(8,128)S(1)} %get-tuple-element.91, f32[1024]{0:T(1024)S(1)} %get-tuple-element.82), kind=kOutput, calls=%fused_computation.27 | convolution fusion | flops 1075314688 | bytes 6295552 | tf_op jit(solution)/shard_map/dot_general | solution.py:144
  150.9 112.4 %all-reduce.5.cloned.1.call-done = (f32[512,256]{0,1:T(8,128)}, f32[128,256]{0,1:T(8,128)}, f32[256,1024]{1,0:T(8,128)}, f32[1024,256]{0,1:T(8,128)}) async-done(((f32[512,256]{0,1:T(8,128)}, f32[128,256]{0,1:T(8,128)}, f32[256,1024]{1,0:T(8,128)}, f32[1024,256]{0,1:T(8,128)}), (f32[512,256]{0,1:T(8,128)}, f32[128,256]{0,1:T(8,128)}, f32[256,1024]{1,0:T(8,128)}, ...) | async-done | bytes 2752528 | tf_op jit(solution)/shard_map/psum | solution.py:213
  264.4 3.6 all-to-all-start.5
  268.8 6.2 %all-to-all-done.5 = bf16[32,2,128]{2,1,0:T(2,128)(2,1)S(1)} async-done(((bf16[32,2,128]{2,1,0:T(2,128)(2,1)}), bf16[32,2,128]{2,1,0:T(2,128)(2,1)S(1)}, u32[]{:S(2)}, u32[]{:S(2)}) %all-to-all-start.5) | async-done | bytes 16416 | tf_op jit(solution)/shard_map/all_to_all | solution.py:189
  275.0 2.6 all-to-all-start.4
  278.6 6.4 %all-to-all-done.4 = bf16[32,8,128]{2,1,0:T(8,128)(2,1)S(1)} async-done(((bf16[32,8,128]{2,1,0:T(8,128)(2,1)}), bf16[32,8,128]{2,1,0:T(8,128)(2,1)S(1)}, u32[]{:S(2)}, u32[]{:S(2)}) %all-to-all-start.4) | async-done | bytes 65568 | tf_op jit(solution)/shard_map/all_to_all | solution.py:180
  285.0 2.6 all-to-all-start.3
  287.8 37.4 %psum.74 = f32[32,256]{1,0:T(8,128)S(1)} all-reduce(f32[32,256]{1,0:T(8,128)S(1)} %fusion.27), channel_id=1, replica_groups=mesh['group'=4,'rep'=8] {'rep'}, use_global_device_ids=true, to_apply=%region_18.19 | all-reduce | flops 8192 | bytes 65536 | tf_op jit(solution)/shard_map/psum | solution.py:213
  325.1 11.2 %psum.75 = f32[32,256]{1,0:T(8,128)S(1)} all-reduce(f32[32,256]{1,0:T(8,128)S(1)} %psum.74), channel_id=1, replica_groups=mesh['group'=4,'rep'=8] {'group'}, use_global_device_ids=true, to_apply=%region_19.20 | all-reduce | flops 8192 | bytes 65536 | tf_op jit(solution)/shard_map/psum | solution.py:213
  338.6 3.0 scatter_custom_fusion.3
  341.6 3.0 scatter_custom_fusion.2
  344.6 3.7 scatter_custom_fusion.1
  350.0 4.5 %all-reduce.7.cloned.1.call-done = (f32[512,256]{0,1:T(8,128)}, f32[128,256]{0,1:T(8,128)}, f32[256,1024]{1,0:T(8,128)}, f32[1024,256]{0,1:T(8,128)}) async-done(((f32[512,256]{0,1:T(8,128)}, f32[128,256]{0,1:T(8,128)}, f32[256,1024]{1,0:T(8,128)}, f32[1024,256]{0,1:T(8,128)}), (f32[512,256]{0,1:T(8,128)}, f32[128,256]{0,1:T(8,128)}, f32[256,1024]{1,0:T(8,128)}, ...) | async-done | bytes 2752528 | tf_op jit(solution)/shard_map/psum | solution.py:213
  (143 shorter events, 40.9 us)
Async XLA Ops:
  7.2 17.5 %copy-start = (bf16[1024,512]{1,0:T(8,128)(2,1)S(1)}, bf16[1024,512]{1,0:T(8,128)(2,1)}, u32[]{:S(2)}) copy-start(bf16[1024,512]{1,0:T(8,128)(2,1)} %param.15) | copy-start | bytes 3145732
  7.2 35.7 %copy-start.26 = (s32[512]{0:T(512)S(1)}, s32[512]{0:T(512)}, u32[]{:S(2)}) copy-start(s32[512]{0:T(512)} %param.24) | copy-start | bytes 6148
  7.2 41.0 %copy-start.20 = (bf16[32,256]{1,0:T(8,128)(2,1)S(1)}, bf16[32,256]{1,0:T(8,128)(2,1)}, u32[]{:S(2)}) copy-start(bf16[32,256]{1,0:T(8,128)(2,1)} %param.20) | copy-start | bytes 49156
  7.2 41.2 %copy-start.16 = (bf16[128,256]{1,0:T(8,128)(2,1)S(1)}, bf16[128,256]{1,0:T(8,128)(2,1)}, u32[]{:S(2)}) copy-start(bf16[128,256]{1,0:T(8,128)(2,1)} %param.19) | copy-start | bytes 196612
  7.2 45.5 %copy-start.9 = (bf16[512,256]{1,0:T(8,128)(2,1)S(1)}, bf16[512,256]{1,0:T(8,128)(2,1)}, u32[]{:S(2)}) copy-start(bf16[512,256]{1,0:T(8,128)(2,1)} %param.18) | copy-start | bytes 786436
  7.2 71.8 %all-gather.6.cloned.1.call-start = ((), (), s32[]{:S(2)}) async-start(), calls=%async_computation.7 | async-start | bytes 1310720 | tf_op jit(solution)/shard_map/all_gather | solution.py:121
  8.7 4.4 %copy-start.25 = (s32[256,1]{0,1:T(1,128)}, s32[256,1]{0,1:T(1,128)S(1)}, u32[]{:S(2)}) copy-start(s32[256,1]{0,1:T(1,128)S(1)} %get-tuple-element.84) | copy-start | bytes 3076
  8.7 13.2 %copy-start.24 = (s32[256,1]{0,1:T(1,128)}, s32[256,1]{0,1:T(1,128)S(1)}, u32[]{:S(2)}) copy-start(s32[256,1]{0,1:T(1,128)S(1)} %get-tuple-element.85) | copy-start | bytes 3076
  8.7 34.2 %copy-start.23 = (s32[256,1]{0,1:T(1,128)}, s32[256,1]{0,1:T(1,128)S(1)}, u32[]{:S(2)}) copy-start(s32[256,1]{0,1:T(1,128)S(1)} %get-tuple-element.83) | copy-start | bytes 3076
  13.1 14.4 %all-to-all-start.2 = ((bf16[32,2,128]{2,1,0:T(2,128)(2,1)}), bf16[32,2,128]{2,1,0:T(2,128)(2,1)S(1)}, u32[]{:S(2)}, u32[]{:S(2)}) async-start(bf16[32,2,128]{2,1,0:T(2,128)(2,1)} %reshape.345), calls=%async_computation.2 | async-start | bytes 32768 | tf_op jit(solution)/shard_map/all_to_all | solution.py:97
  27.5 12.2 %all-to-all-start.1 = ((bf16[32,8,128]{2,1,0:T(8,128)(2,1)}), bf16[32,8,128]{2,1,0:T(8,128)(2,1)S(1)}, u32[]{:S(2)}, u32[]{:S(2)}) async-start(bf16[32,8,128]{2,1,0:T(8,128)(2,1)} %bitcast.9), calls=%async_computation.1 | async-start | bytes 131072 | tf_op jit(solution)/shard_map/all_to_all | solution.py:90
  39.6 13.3 %copy-start.13 = (bf16[32,8,128]{2,1,0:T(8,128)(2,1)}, bf16[32,8,128]{2,1,0:T(8,128)(2,1)S(1)}, u32[]{:S(2)}) copy-start(bf16[32,8,128]{2,1,0:T(8,128)(2,1)S(1)} %all-to-all-done.1) | copy-start | bytes 196612
  39.7 13.0 %all-to-all-start = ((bf16[32,8,512]{2,1,0:T(8,128)(2,1)}), bf16[32,8,512]{2,1,0:T(8,128)(2,1)S(1)}, u32[]{:S(2)}, u32[]{:S(2)}) async-start(bf16[32,8,512]{2,1,0:T(8,128)(2,1)} %bitcast.5), calls=%async_computation | async-start | bytes 524288 | tf_op jit(solution)/shard_map/all_to_all | solution.py:89
  42.2 221.1 %all-reduce.5.cloned.1.call-start = ((), (), s32[]{:S(2)}) async-start(), calls=%async_computation.9 | async-start | bytes 5505024 | tf_op jit(solution)/shard_map/psum | solution.py:213
  48.1 38.7 %copy-start.18 = (s32[4,1,512]{2,1,0:T(1,128)}, s32[4,1,512]{2,1,0:T(1,128)S(1)}, u32[]{:S(2)}) copy-start(s32[4,1,512]{2,1,0:T(1,128)S(1)} %all-gather.3) | copy-start | bytes 24580
  48.2 4.7 %copy-start.11 = (bf16[256,32]{1,0:T(8,128)(2,1)}, bf16[256,32]{1,0:T(8,128)(2,1)S(1)}, u32[]{:S(2)}) copy-start(bf16[256,32]{1,0:T(8,128)(2,1)S(1)} %reshape.346) | copy-start | bytes 49156
  72.5 5.8 %copy-start.14 = (bf16[1024,256]{1,0:T(8,128)(2,1)S(1)}, bf16[1024,256]{1,0:T(8,128)(2,1)}, u32[]{:S(2)}) copy-start(bf16[1024,256]{1,0:T(8,128)(2,1)} %param.22) | copy-start | bytes 1572868
  81.6 7.9 %copy-start.1 = (f32[1024,2048]{1,0:T(8,128)}, f32[1024,2048]{1,0:T(8,128)S(1)}, u32[]{:S(2)}) copy-start(f32[1024,2048]{1,0:T(8,128)S(1)} %get-tuple-element.93) | copy-start | bytes 25165828
  100.5 4.8 %copy-start.19 = (f32[2048]{0:T(1024)}, f32[2048]{0:T(1024)S(1)}, u32[]{:S(2)}) copy-start(f32[2048]{0:T(1024)S(1)} %log_add_fusion) | copy-start | bytes 24580
  100.5 4.8 %copy-start.8 = (bf16[2048,256]{1,0:T(8,128)(2,1)S(1)}, bf16[2048,256]{1,0:T(8,128)(2,1)}, u32[]{:S(2)}) copy-start(bf16[2048,256]{1,0:T(8,128)(2,1)} %all-gather.6.cloned.1.call-done) | copy-start | bytes 3145732
  105.3 3.7 %copy-start.27 = (f32[1024,1024]{1,0:T(8,128)S(1)}, f32[1024,1024]{1,0:T(8,128)}, u32[]{:S(2)}) copy-start(f32[1024,1024]{1,0:T(8,128)} %get-tuple-element.89) | copy-start | bytes 12582916
  115.4 27.9 %copy-start.7 = (bf16[32,8,512]{2,1,0:T(8,128)(2,1)S(1)}, bf16[32,8,512]{2,1,0:T(8,128)(2,1)}, u32[]{:S(2)}) copy-start(bf16[32,8,512]{2,1,0:T(8,128)(2,1)} %copy-done.6) | copy-start | bytes 786436
  146.2 117.2 %copy-start.21 = (bf16[32,256]{1,0:T(8,128)(2,1)S(1)}, bf16[32,256]{1,0:T(8,128)(2,1)}, u32[]{:S(2)}) copy-start(bf16[32,256]{1,0:T(8,128)(2,1)} %param.20) | copy-start | bytes 49156
  146.2 202.0 %reduce-scatter.2.cloned.1.call-start = ((), (), s32[]{:S(2)}) async-start(), calls=%async_computation.8 | async-start | bytes 1310720 | tf_op jit(solution)/shard_map/reduce_scatter | solution.py:143
  150.8 117.2 %copy-start.17 = (bf16[128,256]{1,0:T(8,128)(2,1)S(1)}, bf16[128,256]{1,0:T(8,128)(2,1)}, u32[]{:S(2)}) copy-start(bf16[128,256]{1,0:T(8,128)(2,1)} %param.19) | copy-start | bytes 196612
  150.8 126.8 %copy-start.10 = (bf16[512,256]{1,0:T(8,128)(2,1)S(1)}, bf16[512,256]{1,0:T(8,128)(2,1)}, u32[]{:S(2)}) copy-start(bf16[512,256]{1,0:T(8,128)(2,1)} %param.18) | copy-start | bytes 786436
  150.8 136.8 %copy-start.12 = (bf16[256,32]{1,0:T(8,128)(2,1)S(1)}, bf16[256,32]{1,0:T(8,128)(2,1)}, u32[]{:S(2)}) copy-start(bf16[256,32]{1,0:T(8,128)(2,1)} %copy-done.11) | copy-start | bytes 49156
  150.8 187.7 %copy-start.22 = (f32[256,4]{0,1:T(4,128)S(1)}, f32[256,4]{0,1:T(4,128)}, u32[]{:S(2)}) copy-start(f32[256,4]{0,1:T(4,128)} %get-tuple-element.86) | copy-start | bytes 12292
  150.8 203.7 %all-reduce.7.cloned.1.call-start = ((), (), s32[]{:S(2)}) async-start(), calls=%async_computation.10 | async-start | bytes 5505024 | tf_op jit(solution)/shard_map/psum | solution.py:213
  264.4 10.7 %all-to-all-start.5 = ((bf16[32,2,128]{2,1,0:T(2,128)(2,1)}), bf16[32,2,128]{2,1,0:T(2,128)(2,1)S(1)}, u32[]{:S(2)}, u32[]{:S(2)}) async-start(bf16[32,2,128]{2,1,0:T(2,128)(2,1)} %convert_element_type.98), calls=%async_computation.6 | async-start | bytes 32768 | tf_op jit(solution)/shard_map/all_to_all | solution.py:189
  275.0 10.0 %all-to-all-start.4 = ((bf16[32,8,128]{2,1,0:T(8,128)(2,1)}), bf16[32,8,128]{2,1,0:T(8,128)(2,1)S(1)}, u32[]{:S(2)}, u32[]{:S(2)}) async-start(bf16[32,8,128]{2,1,0:T(8,128)(2,1)} %fusion.10), calls=%async_computation.5 | async-start | bytes 131072 | tf_op jit(solution)/shard_map/all_to_all | solution.py:180
  285.0 59.6 %all-to-all-start.3 = ((bf16[32,8,512]{2,1,0:T(8,128)(2,1)}), bf16[32,8,512]{2,1,0:T(8,128)(2,1)S(1)}, u32[]{:S(2)}, u32[]{:S(2)}) async-start(bf16[32,8,512]{2,1,0:T(8,128)(2,1)} %fusion.9), calls=%async_computation.4 | async-start | bytes 524288 | tf_op jit(solution)/shard_map/all_to_all | solution.py:171
  (6 other events, 9.8 us)
Sparse Core Ops, SparseCore 0:
  9.6 19.5 all-gather.5
  146.3 116.9 all-reduce.4
  265.8 24.0 reduce-scatter.1
  292.4 62.0 all-reduce.6
